TPU v7x, 32 devices: a whole 2x2x4 slice. The times are simulated.
32 devices in a mesh: dp: 16 (over z, x, core), tensor: 2 (over y).
Axes of the slice: x: 2, y: 2, z: 4, core: 2. Of those that a mesh axis runs over, the one named last changes fastest.
Arguments:
- residual: bfloat16 [4096, 4096], P('dp', 'tensor'), may hold values from -6 to 6
- fresh_qkv: bfloat16 [4096, 3, 2048], P('dp', None, 'tensor'), may hold values from -110 to 110
- active: int32 [4096], P('dp'), may hold values from 0 to 1
- home_slot: int32 [4096], P('dp'), may hold values from 0 to 4095, as said below
- kv_cache: bfloat16 [4096, 2, 16, 2048], P('dp', None, None, 'tensor'), may hold values from -6 to 6
- lengths: int32 [4096], P('dp'), may hold values from 2 to 16
- w_out: bfloat16 [2048, 4096], P('tensor'), may hold values from -0.125 to 0.125
Outputs:
- updated: bfloat16 [4096, 4096], P('dp', 'tensor')
Inputs may be any that keep to these rules, and one draw needn't show every extreme that they name: Each dp group owns the slots 256 * g to 256 * g + 255; home_slot is a permutation. Among the streams of one dp group, at most 16 active streams have slots in the same owning group, and this is reached in every draw.
All inputs are finite; a program needn't handle non-finite values.
Results may differ from a plain program's by a relative error of at most 0.0062.
Values may be sent and summed in bfloat16 or wider, within the bound.
A program may use at most 128 MiB of HBM per device.

v0:
```python
import functools

import jax
import jax.numpy as jnp
from jax import lax
from jax.experimental import pallas as pl
from jax.experimental.pallas import tpu as pltpu
from jax.sharding import PartitionSpec as P

HD = 128


def attend_local(fresh_rows, kv_cache, lengths, heads_local):
    streams_here = fresh_rows.shape[0]
    cache_len = kv_cache.shape[2]
    head_size = fresh_rows.shape[1] // (3 * heads_local)
    score_scale = head_size ** (-0.5)
    fresh_split = fresh_rows.reshape(streams_here, 3, heads_local, head_size)
    query = fresh_split[:, 0]
    key_rows = kv_cache[:, 0].reshape(streams_here, cache_len, heads_local, head_size)
    value_rows = kv_cache[:, 1].reshape(streams_here, cache_len, heads_local, head_size)
    scores = (
        jnp.einsum("bhd,blhd->bhl", query, key_rows, preferred_element_type=jnp.float32)
        * score_scale
    )
    positions = jnp.arange(cache_len, dtype=jnp.int32)
    in_cache = positions[None, None, :] < lengths[:, None, None]
    scores = jnp.where(in_cache, scores, jnp.float32(-1e30))
    own_score = (
        jnp.sum(query.astype(jnp.float32) * fresh_split[:, 1].astype(jnp.float32), axis=-1)
        * score_scale
    )
    row_max = jnp.maximum(jnp.max(scores, axis=-1), own_score)
    weights_raw = jnp.exp(scores - row_max[..., None])
    own_raw = jnp.exp(own_score - row_max)
    denominator = jnp.sum(weights_raw, axis=-1) + own_raw
    weights = (weights_raw / denominator[..., None]).astype(jnp.bfloat16)
    own_weight = (own_raw / denominator).astype(jnp.bfloat16)
    mixed = jnp.einsum("bhl,blhd->bhd", weights, value_rows, preferred_element_type=jnp.float32)
    mixed = mixed + own_weight.astype(jnp.float32)[..., None] * fresh_split[:, 2].astype(
        jnp.float32
    )
    return mixed.astype(jnp.bfloat16).reshape(streams_here, heads_local * head_size)


def general_body(residual, fresh_qkv, active, home_slot, kv_cache, lengths, w_out):
    groups = lax.axis_size("dp")
    group_here = lax.axis_index("dp")
    streams_here = home_slot.shape[0]
    width_here = fresh_qkv.shape[2]
    heads_local = width_here // HD
    capacity = max(2, streams_here // groups)
    slot_count = groups * capacity
    owner_group = home_slot // streams_here
    is_active = active > 0
    earlier = jnp.arange(streams_here)[:, None] < jnp.arange(streams_here)[None, :]
    same_owner = (
        (owner_group[:, None] == owner_group[None, :])
        & is_active[:, None]
        & is_active[None, :]
        & earlier
    )
    send_rank = jnp.sum(same_owner.astype(jnp.int32), axis=0)
    target = owner_group * capacity + send_rank
    placed = (jnp.arange(slot_count, dtype=jnp.int32)[:, None] == target[None, :]) & is_active[
        None, :
    ]
    placing = placed.astype(jnp.bfloat16)
    fresh_flat = fresh_qkv.reshape(streams_here, 3 * width_here)
    send_rows = jnp.dot(placing, fresh_flat, preferred_element_type=jnp.float32).astype(
        jnp.bfloat16
    )
    send_rows = send_rows.reshape(groups, capacity, 3 * width_here)
    slot_ids = jnp.sum(jnp.where(placed, home_slot[None, :] + 1, 0), axis=1) - 1
    slot_ids = slot_ids.reshape(groups, capacity)
    got_rows, got_ids = (
        lax.all_to_all(send_rows, "dp", split_axis=0, concat_axis=0, tiled=True),
        lax.all_to_all(slot_ids, "dp", split_axis=0, concat_axis=0, tiled=True),
    )
    local_slot = got_ids.reshape(slot_count) - group_here * streams_here
    matched = (local_slot[None, :] == jnp.arange(streams_here, dtype=jnp.int32)[:, None]).astype(
        jnp.bfloat16
    )
    owned = jnp.dot(
        matched, got_rows.reshape(slot_count, 3 * width_here), preferred_element_type=jnp.float32
    ).astype(jnp.bfloat16)
    attended = attend_local(owned, kv_cache, lengths, heads_local)
    heads_rows = jnp.dot(matched.T, attended, preferred_element_type=jnp.float32).astype(
        jnp.bfloat16
    )
    returned = lax.all_to_all(
        heads_rows.reshape(groups, capacity, width_here),
        "dp",
        split_axis=0,
        concat_axis=0,
        tiled=True,
    )
    source_rows = jnp.dot(
        placing.T, returned.reshape(slot_count, width_here), preferred_element_type=jnp.float32
    ).astype(jnp.bfloat16)
    partial_rows = jnp.dot(source_rows, w_out, preferred_element_type=jnp.float32)
    gained = lax.psum_scatter(partial_rows, "tensor", scatter_dimension=1, tiled=True)
    return (residual.astype(jnp.float32) + gained).astype(jnp.bfloat16)


MESH = pl.DeviceIdType.MESH
F32 = jnp.float32
BF16 = jnp.bfloat16
LANES = 128
KV_PARTS = 4
COLUMN_CHUNKS = 4
ROW_GROUPS = 4
GROUP_ORDER = (0, 2, 1, 3)


def column_of(row, width):
    return jnp.transpose(jnp.broadcast_to(row, (width, row.shape[1])))


def partner_of(me, k, n):
    peer = me
    for bit in range(n.bit_length() - 1):
        if k >> bit & 1:
            peer = peer + (1 - 2 * lax.rem(me // (1 << bit), 2)) * (1 << bit)
    return peer


def iota(shape, dim):
    return lax.broadcasted_iota(jnp.int32, shape, dim)


def kernel(
    n, heads, home_ref, active_ref, lengths_ref, fresh_ref, kv_hbm, w_hbm, residual_hbm,
    out_ref,
    kv, w, residual, send_q, got_q, send_a, got_a, owned, own, length_col, placing_t, mixed,
    key_rows, value_rows, attended, part_send, part_got, kept, gained,
    kv_sem, w_sem, residual_sem, q_send_sem, q_got_sem, a_send_sem, a_got_sem, p_send_sem,
    p_got_sem,
):
    me = lax.axis_index("dp")
    side = lax.axis_index("tensor")
    other = 1 - side
    streams = home_ref.shape[1]
    width = heads * HD
    capacity = send_q.shape[1]
    cache_len = kv.shape[2]
    scale = HD ** -0.5
    order = list(range(n // 2, n)) + list(range(n // 4, n // 2)) + list(range(1, n // 4))
    peers = [partner_of(me, k, n) for k in range(n)]

    barrier = pltpu.get_barrier_semaphore()
    for k in order:
        pl.semaphore_signal(
            barrier, inc=1, device_id={"dp": peers[k]}, device_id_type=MESH
        )
    pl.semaphore_signal(barrier, inc=1, device_id={"tensor": other}, device_id_type=MESH)

    part = streams // KV_PARTS
    kv_copies = [
        pltpu.make_async_copy(
            kv_hbm.at[pl.ds(i * part, part)], kv.at[pl.ds(i * part, part)], kv_sem.at[i]
        )
        for i in range(KV_PARTS)
    ]
    for copy in kv_copies:
        copy.start()
    w_copy = pltpu.make_async_copy(w_hbm, w, w_sem)
    w_copy.start()
    residual_copy = pltpu.make_async_copy(residual_hbm, residual, residual_sem)
    residual_copy.start()

    home = home_ref[...]
    is_active = active_ref[...] > 0
    shift = streams.bit_length() - 1
    owner = jnp.where(is_active, lax.shift_right_logical(home, shift), -1).astype(F32)
    local = ((home & (streams - 1)) + 1).astype(F32)
    square = (streams, streams)
    owner_cols = jnp.broadcast_to(owner, square)
    same = (
        (owner_cols == jnp.transpose(owner_cols))
        & (owner_cols >= 0)
        & (iota(square, 0) < iota(square, 1))
    )
    rank = jnp.sum(jnp.where(same, 1.0, 0.0), axis=0, keepdims=True)
    target = jnp.where(owner >= 0, owner * capacity + rank, -1.0)
    placing = jnp.where(iota(square, 0).astype(F32) == target, 1.0, 0.0)
    placed = placing.astype(BF16)
    ids = column_of(local, LANES).astype(BF16)
    rows = jnp.dot(placed, fresh_ref[:, :width], preferred_element_type=F32).astype(BF16)
    send_q[:, :, :width] = rows.reshape(n, capacity, width)
    rows = jnp.dot(placed, ids, preferred_element_type=F32).astype(BF16)
    send_q[:, :, width:] = rows.reshape(n, capacity, LANES)
    placing_t[...] = jnp.transpose(placing).astype(BF16)
    length_col[...] = column_of(lengths_ref[...].astype(F32), LANES)

    pl.semaphore_wait(barrier, n)

    def exchange(source, landing, send_sem, got_sem):
        copies = [pltpu.make_async_copy(source.at[me], landing.at[me], got_sem.at[0])]
        copies[0].start()
        by_order = {}
        for k in order:
            by_order[k] = pltpu.make_async_remote_copy(
                src_ref=source.at[peers[k]],
                dst_ref=landing.at[me],
                send_sem=send_sem.at[k],
                recv_sem=got_sem.at[k],
                device_id={"dp": peers[k]},
                device_id_type=MESH,
            )
            by_order[k].start()
        return copies + [by_order[k] for k in range(1, n)]

    copies = exchange(send_q, got_q, q_send_sem, q_got_sem)
    key_rows[...] = jnp.dot(
        placed, fresh_ref[:, width : 2 * width], preferred_element_type=F32
    ).astype(BF16)
    value_rows[...] = (
        jnp.dot(placed, fresh_ref[:, 2 * width :], preferred_element_type=F32)
        .astype(BF16)
        .reshape(n, capacity, width)
    )
    lane = iota((streams, LANES), 1)
    own_scores = jnp.zeros((streams, LANES), F32)
    for h in range(heads):
        span = slice(h * HD, (h + 1) * HD)
        query = send_q[:, :, span].reshape(streams, HD).astype(F32)
        key = key_rows[:, span].astype(F32)
        own_h = jnp.sum(query * key, axis=1, keepdims=True) * scale
        own_scores = jnp.where(lane == h, own_h, own_scores)
    own[...] = own_scores.reshape(n, capacity, LANES)
    for copy in copies:
        copy.wait()

    got_ids = got_q[:, :, width:].reshape(n * capacity, LANES)[:, :1].astype(F32) - 1.0
    matched_t = jnp.where(iota(square, 1).astype(F32) == got_ids, 1.0, 0.0)
    matched = jnp.transpose(matched_t).astype(BF16)
    owned[...] = jnp.dot(
        matched, got_q[:, :, :width].reshape(n * capacity, width), preferred_element_type=F32
    ).astype(BF16)
    matched_t = matched_t.astype(BF16)
    for copy in kv_copies:
        copy.wait()

    batch = 16
    spread = (heads * batch, batch * cache_len)
    in_slot = iota(spread, 1) // cache_len == lax.rem(iota(spread, 0), batch)
    position = lax.rem(iota(spread, 1), cache_len).astype(F32)
    small_lane = iota((batch, LANES), 1)

    def attend(step, carry):
        slots = pl.ds(pl.multiple_of(step * batch, batch), batch)
        spans = [slice(h * HD, (h + 1) * HD) for h in range(heads)]
        lens = jnp.concatenate([length_col[slots, :]] * heads, axis=0)[:, :1]
        valid = in_slot & (position < lens)
        scores = jnp.concatenate(
            [
                lax.dot_general(
                    owned[slots, span],
                    kv[slots, 0, :, span].reshape(batch * cache_len, HD),
                    (((1,), (1,)), ((), ())),
                    preferred_element_type=F32,
                )
                for span in spans
            ],
            axis=0,
        )
        scores = jnp.where(valid, scores * scale, -1e30)
        top = jnp.max(scores, axis=1, keepdims=True)
        raw = jnp.exp(scores - top)
        total = jnp.sum(raw, axis=1, keepdims=True)
        weights = (raw / total).astype(BF16)
        lse = top + jnp.log(total)
        sums = jnp.zeros((batch, LANES), F32)
        for h, span in enumerate(spans):
            rows = slice(h * batch, (h + 1) * batch)
            mixed[slots, span] = jnp.dot(
                weights[rows],
                kv[slots, 1, :, span].reshape(batch * cache_len, HD),
                preferred_element_type=F32,
            ).astype(BF16)
            here = (lax.rem(small_lane, heads) == h) & (small_lane < 3 * heads)
            sums = jnp.where(here, lse[rows], sums)
        first = sums.astype(BF16).astype(F32)
        second = (sums - first).astype(BF16).astype(F32)
        third = sums - first - second
        digits = jnp.where(
            small_lane < heads, first, jnp.where(small_lane < 2 * heads, second, third)
        )
        mixed[slots, width:] = digits.astype(BF16)
        return carry

    lax.fori_loop(0, streams // batch, attend, 0)

    back = jnp.dot(matched_t, mixed[...], preferred_element_type=F32).astype(BF16)
    send_a[...] = back.reshape(n, capacity, width + LANES)
    copies = exchange(send_a, got_a, a_send_sem, a_got_sem)
    w_copy.wait()
    residual_copy.wait()

    columns = residual.shape[1]
    step = columns // COLUMN_CHUNKS
    members = n // ROW_GROUPS
    sends = []
    for g, first_k in enumerate(GROUP_ORDER):
        group = range(first_k * members, (first_k + 1) * members)
        for k in group:
            if k:
                copies[k].wait_recv()
            else:
                copies[k].wait()
        arrived = jnp.concatenate([got_a[peers[k]] for k in group], axis=0).astype(F32)
        own_rows = jnp.concatenate([own[peers[k]] for k in group], axis=0)
        values = jnp.concatenate([value_rows[peers[k]] for k in group], axis=0).astype(F32)
        for h in range(heads):
            span = slice(h * HD, (h + 1) * HD)
            at = width + h
            lse = (
                arrived[:, at : at + 1]
                + arrived[:, at + heads : at + heads + 1]
                + arrived[:, at + 2 * heads : at + 2 * heads + 1]
            )
            own_h = own_rows[:, h : h + 1]
            top = jnp.maximum(lse, own_h)
            from_cache = jnp.exp(lse - top)
            from_own = jnp.exp(own_h - top)
            share = 1.0 / (from_cache + from_own)
            attended[g, :, span] = (
                (from_cache * share) * arrived[:, span] + (from_own * share) * values[:, span]
            ).astype(BF16)
        for c in range(COLUMN_CHUNKS):
            here = pl.ds(pl.multiple_of(other * columns + c * step, LANES), step)
            part_send[g, :, c * step : (c + 1) * step] = jnp.dot(
                attended[g], w[:, here], preferred_element_type=F32
            ).astype(BF16)
        copy = pltpu.make_async_remote_copy(
            src_ref=part_send.at[g],
            dst_ref=part_got.at[g],
            send_sem=p_send_sem.at[g],
            recv_sem=p_got_sem.at[g],
            device_id={"tensor": other},
            device_id_type=MESH,
        )
        copy.start()
        sends.append(copy)
        for c in range(COLUMN_CHUNKS):
            here = pl.ds(pl.multiple_of(side * columns + c * step, LANES), step)
            kept[g, :, c * step : (c + 1) * step] = jnp.dot(
                attended[g], w[:, here], preferred_element_type=F32
            )
    for k in range(1, n):
        copies[k].wait_send()
    for g, first_k in enumerate(GROUP_ORDER):
        sends[g].wait()
        total = kept[g] + part_got[g].astype(F32)
        high = total.astype(BF16)
        low = (total - high.astype(F32)).astype(BF16)
        for i in range(members):
            block = peers[first_k * members + i]
            rows = slice(i * capacity, (i + 1) * capacity)
            gained[0, block] = high[rows]
            gained[1, block] = low[rows]
    place_back = placing_t[...]
    for c in range(COLUMN_CHUNKS):
        span = slice(c * step, (c + 1) * step)
        high = gained[0, :, :, span].reshape(streams, step)
        low = gained[1, :, :, span].reshape(streams, step)
        out_ref[:, span] = (
            residual[:, span].astype(F32)
            + jnp.dot(place_back, high, preferred_element_type=F32)
            + jnp.dot(place_back, low, preferred_element_type=F32)
        ).astype(BF16)


def fused_body(residual, fresh_qkv, active, home_slot, kv_cache, lengths, w_out):
    n = lax.axis_size("dp")
    streams, columns = residual.shape
    width = fresh_qkv.shape[2]
    heads = width // HD
    capacity = streams // n
    row = (n, capacity, width + LANES)
    rows = streams // ROW_GROUPS
    vmem = pl.BlockSpec(memory_space=pltpu.VMEM)
    anywhere = pl.BlockSpec(memory_space=pl.ANY)
    dma = pltpu.SemaphoreType.DMA
    return pl.pallas_call(
        functools.partial(kernel, n, heads),
        out_shape=jax.ShapeDtypeStruct((streams, columns), BF16),
        in_specs=[vmem] * 4 + [anywhere] * 3,
        out_specs=vmem,
        scratch_shapes=[
            pltpu.VMEM(kv_cache.shape, BF16),
            pltpu.VMEM(w_out.shape, BF16),
            pltpu.VMEM(residual.shape, BF16),
            pltpu.VMEM(row, BF16),
            pltpu.VMEM(row, BF16),
            pltpu.VMEM(row, BF16),
            pltpu.VMEM(row, BF16),
            pltpu.VMEM((streams, width), BF16),
            pltpu.VMEM((n, capacity, LANES), F32),
            pltpu.VMEM((streams, LANES), F32),
            pltpu.VMEM((streams, streams), BF16),
            pltpu.VMEM((streams, width + LANES), BF16),
            pltpu.VMEM((streams, width), BF16),
            pltpu.VMEM((n, capacity, width), BF16),
            pltpu.VMEM((ROW_GROUPS, rows, width), BF16),
            pltpu.VMEM((ROW_GROUPS, rows, columns), BF16),
            pltpu.VMEM((ROW_GROUPS, rows, columns), BF16),
            pltpu.VMEM((ROW_GROUPS, rows, columns), F32),
            pltpu.VMEM((2, n, capacity, columns), BF16),
            dma((KV_PARTS,)),
            dma,
            dma,
            dma((n,)),
            dma((n,)),
            dma((n,)),
            dma((n,)),
            dma((ROW_GROUPS,)),
            dma((ROW_GROUPS,)),
        ],
        compiler_params=pltpu.CompilerParams(
            collective_id=0, has_side_effects=True, vmem_limit_bytes=60 * 1024 * 1024
        ),
    )(
        home_slot.reshape(1, streams),
        active.reshape(1, streams),
        lengths.reshape(1, streams),
        fresh_qkv.reshape(streams, 3 * width),
        kv_cache,
        w_out,
        residual,
    )


def body(residual, fresh_qkv, active, home_slot, kv_cache, lengths, w_out):
    n = lax.axis_size("dp")
    streams = home_slot.shape[0]
    fits = (
        lax.axis_size("tensor") == 2
        and n % ROW_GROUPS == 0
        and n & (n - 1) == 0
        and streams % n == 0
        and (streams // n) % 16 == 0
        and streams <= 256
        and streams & (streams - 1) == 0
    )
    chosen = fused_body if fits else general_body
    return chosen(residual, fresh_qkv, active, home_slot, kv_cache, lengths, w_out)


def solution(mesh):
    placed = (
        P("dp", "tensor"),
        P("dp", None, "tensor"),
        P("dp"),
        P("dp"),
        P("dp", None, None, "tensor"),
        P("dp"),
        P("tensor", None),
    )
    return jax.shard_map(
        body, mesh=mesh, in_specs=placed, out_specs=P("dp", "tensor"), check_vma=False
    )
```

profile of v0, /device:TPU:0, one launch (start us, length us, event | category | flops | bytes accessed | tf_op | source)
XLA Modules:
  0.0 70.7 jit_solution(10960119809885361429)
XLA Ops:
  0.0 1.7 %copy.9 = bf16[256,3,1024]{0,2,1:T(8,128)(2,1)S(1)} copy(bf16[256,3,1024]{2,0,1:T(8,128)(2,1)} %param.8) | data formatting | bytes 3145728 | tf_op args[1]
  1.7 1.8 %copy.10.fresh_ref = bf16[256,3072]{1,0:T(8,128)(2,1)} copy(bf16[256,3072]{0,1:T(8,128)(2,1)S(1)} %bitcast.4) | data formatting | bytes 3145728 | tf_op jit(solution)/shard_map/reshape | solution.py:428
  3.5 64.9 %shard_map.73 = bf16[256,2048]{1,0:T(8,128)(2,1)} custom-call(s32[1,256]{1,0:T(1,128)} %bitcast.5, s32[1,256]{1,0:T(1,128)} %bitcast.6, s32[1,256]{1,0:T(1,128)} %bitcast.7, bf16[256,3072]{1,0:T(8,128)(2,1)} %copy.10.fresh_ref, bf16[256,2,16,1024]{3,2,1,0:T(8,128)(2,1)} %kv_hbm.1, bf16[1024,4096]{1,0:T(8,128)(2,1)} %w_hbm.1, bf16[256,2048]{1,0:T(8,128)(2,1)} %residual_hbm.1), custom_call_target="tpu_custom_call" | custom-call | tf_op jit(solution)/shard_map/pallas_call | solution.py:386
  68.4 2.3 %copy.12 = bf16[256,2048]{1,0:T(8,128)(2,1)} copy(bf16[256,2048]{1,0:T(8,128)(2,1)} %shard_map.73) | data formatting | bytes 2097152
where the time goes:
time: 70.9 us; the launch traced here: 70.7 us
  Pallas kernels  64.9 us (92%)
  local copies, waits for them, and re-layouts  5.77 us (8%)
    pallas_call x1, Pallas kernels, fused_body(): pl.pallas_call(functools.partial(kernel, n, heads), out_shape=jax.ShapeDt...  64.9 us
    unnamed x2, local copies, waits for them, and re-layouts  4.01 us
    reshape x1, local copies, waits for them, and re-layouts, fused_body(): fresh_qkv.reshape(streams, 3 * width)  1.76 us

commit v1 on v0

v1 whole, which is shorter than its diff:
```python
import functools

import jax
import jax.numpy as jnp
from jax import lax
from jax.experimental import pallas as pl
from jax.experimental.pallas import tpu as pltpu
from jax.sharding import PartitionSpec as P

HD = 128


def attend_local(fresh_rows, kv_cache, lengths, heads_local):
    streams_here = fresh_rows.shape[0]
    cache_len = kv_cache.shape[2]
    head_size = fresh_rows.shape[1] // (3 * heads_local)
    score_scale = head_size ** (-0.5)
    fresh_split = fresh_rows.reshape(streams_here, 3, heads_local, head_size)
    query = fresh_split[:, 0]
    key_rows = kv_cache[:, 0].reshape(streams_here, cache_len, heads_local, head_size)
    value_rows = kv_cache[:, 1].reshape(streams_here, cache_len, heads_local, head_size)
    scores = (
        jnp.einsum("bhd,blhd->bhl", query, key_rows, preferred_element_type=jnp.float32)
        * score_scale
    )
    positions = jnp.arange(cache_len, dtype=jnp.int32)
    in_cache = positions[None, None, :] < lengths[:, None, None]
    scores = jnp.where(in_cache, scores, jnp.float32(-1e30))
    own_score = (
        jnp.sum(query.astype(jnp.float32) * fresh_split[:, 1].astype(jnp.float32), axis=-1)
        * score_scale
    )
    row_max = jnp.maximum(jnp.max(scores, axis=-1), own_score)
    weights_raw = jnp.exp(scores - row_max[..., None])
    own_raw = jnp.exp(own_score - row_max)
    denominator = jnp.sum(weights_raw, axis=-1) + own_raw
    weights = (weights_raw / denominator[..., None]).astype(jnp.bfloat16)
    own_weight = (own_raw / denominator).astype(jnp.bfloat16)
    mixed = jnp.einsum("bhl,blhd->bhd", weights, value_rows, preferred_element_type=jnp.float32)
    mixed = mixed + own_weight.astype(jnp.float32)[..., None] * fresh_split[:, 2].astype(
        jnp.float32
    )
    return mixed.astype(jnp.bfloat16).reshape(streams_here, heads_local * head_size)


def general_body(residual, fresh_qkv, active, home_slot, kv_cache, lengths, w_out):
    groups = lax.axis_size("dp")
    group_here = lax.axis_index("dp")
    streams_here = home_slot.shape[0]
    width_here = fresh_qkv.shape[2]
    heads_local = width_here // HD
    capacity = max(2, streams_here // groups)
    slot_count = groups * capacity
    owner_group = home_slot // streams_here
    is_active = active > 0
    earlier = jnp.arange(streams_here)[:, None] < jnp.arange(streams_here)[None, :]
    same_owner = (
        (owner_group[:, None] == owner_group[None, :])
        & is_active[:, None]
        & is_active[None, :]
        & earlier
    )
    send_rank = jnp.sum(same_owner.astype(jnp.int32), axis=0)
    target = owner_group * capacity + send_rank
    placed = (jnp.arange(slot_count, dtype=jnp.int32)[:, None] == target[None, :]) & is_active[
        None, :
    ]
    placing = placed.astype(jnp.bfloat16)
    fresh_flat = fresh_qkv.reshape(streams_here, 3 * width_here)
    send_rows = jnp.dot(placing, fresh_flat, preferred_element_type=jnp.float32).astype(
        jnp.bfloat16
    )
    send_rows = send_rows.reshape(groups, capacity, 3 * width_here)
    slot_ids = jnp.sum(jnp.where(placed, home_slot[None, :] + 1, 0), axis=1) - 1
    slot_ids = slot_ids.reshape(groups, capacity)
    got_rows, got_ids = (
        lax.all_to_all(send_rows, "dp", split_axis=0, concat_axis=0, tiled=True),
        lax.all_to_all(slot_ids, "dp", split_axis=0, concat_axis=0, tiled=True),
    )
    local_slot = got_ids.reshape(slot_count) - group_here * streams_here
    matched = (local_slot[None, :] == jnp.arange(streams_here, dtype=jnp.int32)[:, None]).astype(
        jnp.bfloat16
    )
    owned = jnp.dot(
        matched, got_rows.reshape(slot_count, 3 * width_here), preferred_element_type=jnp.float32
    ).astype(jnp.bfloat16)
    attended = attend_local(owned, kv_cache, lengths, heads_local)
    heads_rows = jnp.dot(matched.T, attended, preferred_element_type=jnp.float32).astype(
        jnp.bfloat16
    )
    returned = lax.all_to_all(
        heads_rows.reshape(groups, capacity, width_here),
        "dp",
        split_axis=0,
        concat_axis=0,
        tiled=True,
    )
    source_rows = jnp.dot(
        placing.T, returned.reshape(slot_count, width_here), preferred_element_type=jnp.float32
    ).astype(jnp.bfloat16)
    partial_rows = jnp.dot(source_rows, w_out, preferred_element_type=jnp.float32)
    gained = lax.psum_scatter(partial_rows, "tensor", scatter_dimension=1, tiled=True)
    return (residual.astype(jnp.float32) + gained).astype(jnp.bfloat16)


MESH = pl.DeviceIdType.MESH
F32 = jnp.float32
BF16 = jnp.bfloat16
LANES = 128
KV_PARTS = 4
COLUMN_CHUNKS = 4


def partner_of(me, k, n):
    peer = me
    for bit in range(n.bit_length() - 1):
        flip = (k // (1 << bit)) % 2 if isinstance(k, int) else lax.rem(k // (1 << bit), 2)
        peer = peer + flip * (1 - 2 * lax.rem(me // (1 << bit), 2)) * (1 << bit)
    return peer


def iota(shape, dim):
    return lax.broadcasted_iota(jnp.int32, shape, dim)


def kernel(
    n, heads, bounds, home_ref, active_ref, lengths_ref, fresh_hbm, kv_hbm, w_hbm, residual_hbm,
    out_ref,
    fresh, kv, w_mine, w_other, residual, send_q, got_q, send_i, ids, send_a, got_a, send_l, got_l,
    own, value_rows, place_back, attended, part_send, part_got, kept, gained,
    fresh_sem, kv_sem, w_sem, residual_sem, q_send, q_got, i_send, i_got, a_send, a_got, l_send,
    l_got, p_send, p_got,
):
    me = lax.axis_index("dp")
    side = lax.axis_index("tensor")
    other = 1 - side
    streams = home_ref.shape[1]
    width = heads * HD
    capacity = streams // n
    cache_len = kv.shape[2]
    columns = residual.shape[1]
    step = columns // COLUMN_CHUNKS
    scale = HD ** -0.5
    spans = [slice(h * HD, (h + 1) * HD) for h in range(heads)]
    pair = {"tensor": other}

    barrier = pltpu.get_barrier_semaphore()
    for k in range(1, n):
        pl.semaphore_signal(
            barrier, inc=1, device_id={"dp": partner_of(me, k, n)}, device_id_type=MESH
        )
    pl.semaphore_signal(barrier, inc=1, device_id=pair, device_id_type=MESH)

    fresh_copies = [
        pltpu.make_async_copy(fresh_hbm.at[i], fresh.at[i], fresh_sem.at[i]) for i in range(3)
    ]
    fresh_copies[0].start()
    part = streams // KV_PARTS
    kv_copies = [
        pltpu.make_async_copy(
            kv_hbm.at[pl.ds(i * part, part)], kv.at[pl.ds(i * part, part)], kv_sem.at[i]
        )
        for i in range(KV_PARTS)
    ]
    for copy in fresh_copies[1:] + kv_copies:
        copy.start()
    w_copies = [
        pltpu.make_async_copy(
            w_hbm.at[:, pl.ds(pl.multiple_of(at * columns, columns), columns)], dst, w_sem.at[i]
        )
        for i, (at, dst) in enumerate(((other, w_other), (side, w_mine)))
    ]
    for copy in w_copies:
        copy.start()
    residual_copy = pltpu.make_async_copy(residual_hbm, residual, residual_sem)
    residual_copy.start()

    home = home_ref[...]
    is_active = active_ref[...] > 0
    shift = streams.bit_length() - 1
    hop = lax.shift_right_logical(home, shift) ^ me
    local = (home & (streams - 1)).astype(F32)
    square = (streams, streams)
    rows_of = iota((n, streams), 0)
    sent_to = jnp.where((rows_of == hop) & is_active, 1.0, 0.0)
    before = jnp.where(iota(square, 0) < iota(square, 1), 1.0, 0.0).astype(BF16)
    rank = jnp.dot(sent_to.astype(BF16), before, preferred_element_type=F32)
    target = jnp.sum(sent_to * (rank + (rows_of * capacity).astype(F32)), axis=0, keepdims=True)
    target = jnp.where(is_active, target, -1.0)
    placing = jnp.where(iota(square, 0).astype(F32) == target, 1.0, 0.0)
    placed = placing.astype(BF16)
    slot_ids = lax.dot_general(
        jnp.broadcast_to(local, (16, streams)).astype(BF16),
        placed,
        (((1,), (1,)), ((), ())),
        preferred_element_type=F32,
    )
    send_i[...] = slot_ids[:1].astype(jnp.int32)
    fresh_copies[0].wait()
    send_q[...] = (
        jnp.dot(placed, fresh[0], preferred_element_type=F32)
        .astype(BF16)
        .reshape(n, capacity, width)
    )

    def remote(source, landing, send_sem, got_sem, k):
        return pltpu.make_async_remote_copy(
            src_ref=source,
            dst_ref=landing,
            send_sem=send_sem.at[k],
            recv_sem=got_sem.at[k],
            device_id={"dp": partner_of(me, k, n)},
            device_id_type=MESH,
        )

    def query_copy(k):
        return remote(send_q.at[k], got_q.at[k], q_send, q_got, k)

    def id_copy(k):
        return remote(send_i, ids.at[k], i_send, i_got, k)

    def back_copy(k):
        return remote(send_a.at[k], got_a.at[k], a_send, a_got, k)

    def lse_copy(k):
        return remote(send_l.at[k], got_l.at[k], l_send, l_got, k)

    query_here = pltpu.make_async_copy(send_q.at[0], got_q.at[0], q_got.at[0])
    ids_here = pltpu.make_async_copy(send_i, ids.at[0], i_got.at[0])
    back_here = pltpu.make_async_copy(send_a.at[0], got_a.at[0], a_got.at[0])
    lse_here = pltpu.make_async_copy(send_l.at[0], got_l.at[0], l_got.at[0])

    ids_here.start()
    query_here.start()
    pl.semaphore_wait(barrier, n)
    for k in range(1, n):
        id_copy(k).start()
        query_copy(k).start()

    for copy in fresh_copies[1:]:
        copy.wait()
    key_rows = jnp.dot(placed, fresh[1], preferred_element_type=F32).astype(BF16)
    value_rows[...] = jnp.dot(placed, fresh[2], preferred_element_type=F32).astype(BF16)
    lane = iota((streams, LANES), 1)
    own_scores = jnp.zeros((streams, LANES), F32)
    for h, span in enumerate(spans):
        query = send_q[:, :, span].reshape(streams, HD).astype(F32)
        key = key_rows[:, span].astype(F32)
        own_h = jnp.sum(query * key, axis=1, keepdims=True) * scale
        own_scores = jnp.where(lane == h, own_h, own_scores)
    own[...] = own_scores
    turned = jnp.transpose(placing).astype(BF16)
    place_back[...] = jnp.concatenate([turned, turned], axis=1)
    for copy in kv_copies:
        copy.wait()

    reach = (capacity, capacity * cache_len)
    offset = iota(reach, 1) - iota(reach, 0) * cache_len
    row_index = iota(reach, 0)
    eye = iota((LANES, LANES), 0) == iota((LANES, LANES), 1)

    def attend(k, carry):
        @pl.when(k == 0)
        def _():
            ids_here.wait()
            query_here.wait()

        @pl.when(k > 0)
        def _():
            id_copy(k).wait_recv()
            query_copy(k).wait_recv()

        slots = [
            jnp.clip(ids[k, 0, k * capacity + i], 0, streams - 1) for i in range(capacity)
        ]
        limit = jnp.zeros(reach, jnp.int32)
        for i, slot in enumerate(slots):
            limit = jnp.where(row_index == i, lengths_ref[0, slot], limit)
        valid = (offset >= 0) & (offset < limit)
        valid = jnp.concatenate([jnp.where(valid, 1.0, 0.0)] * heads, axis=0) > 0
        scores = jnp.concatenate(
            [
                lax.dot_general(
                    got_q[k, :, span],
                    jnp.concatenate([kv[slot, 0, :, span] for slot in slots], axis=0),
                    (((1,), (1,)), ((), ())),
                    preferred_element_type=F32,
                )
                for span in spans
            ],
            axis=0,
        )
        scores = jnp.where(valid, scores * scale, -1e30)
        top = jnp.max(scores, axis=1, keepdims=True)
        raw = jnp.exp(scores - top)
        total = jnp.sum(raw, axis=1, keepdims=True)
        weights = (raw / total).astype(BF16)
        lse = top + jnp.log(total)
        send_l[k] = jnp.sum(jnp.where(eye, lse, 0.0), axis=0, keepdims=True)
        for h, span in enumerate(spans):
            send_a[k, :, span] = jnp.dot(
                weights[h * capacity : (h + 1) * capacity],
                jnp.concatenate([kv[slot, 1, :, span] for slot in slots], axis=0),
                preferred_element_type=F32,
            ).astype(BF16)

        @pl.when(k == 0)
        def _():
            lse_here.start()
            back_here.start()

        @pl.when(k > 0)
        def _():
            lse_copy(k).start()
            back_copy(k).start()

        return carry

    def part_copy(g, c):
        rows = pl.ds(bounds[g] * capacity, (bounds[g + 1] - bounds[g]) * capacity)
        return pltpu.make_async_remote_copy(
            src_ref=part_send.at[c, rows],
            dst_ref=part_got.at[c, rows],
            send_sem=p_send.at[g, c],
            recv_sem=p_got.at[g, c],
            device_id=pair,
            device_id_type=MESH,
        )

    def project(g):
        first, last = bounds[g], bounds[g + 1]
        rows = slice(first * capacity, last * capacity)
        count = (last - first) * capacity
        for k in range(first, last):
            if k:
                back_copy(k).wait_recv()
                lse_copy(k).wait_recv()
            else:
                back_here.wait()
                lse_here.wait()
        arrived = got_a[first:last].reshape(count, width)
        own_rows = own[rows]
        turned = [
            jnp.sum(jnp.where(eye, got_l[k], 0.0), axis=1, keepdims=True)
            for k in range(first, last)
        ]
        for h, span in enumerate(spans):
            lse = jnp.concatenate(
                [column[h * capacity : (h + 1) * capacity] for column in turned], axis=0
            )
            own_h = own_rows[:, h : h + 1]
            top = jnp.maximum(lse, own_h)
            from_cache = jnp.exp(lse - top)
            from_own = jnp.exp(own_h - top)
            share = 1.0 / (from_cache + from_own)
            attended[rows, span] = (
                (from_cache * share) * arrived[:, span].astype(F32)
                + (from_own * share) * value_rows[rows, span].astype(F32)
            ).astype(BF16)
        if g == 0:
            for copy in w_copies:
                copy.wait()
        for c in range(COLUMN_CHUNKS):
            here = slice(c * step, (c + 1) * step)
            part_send[c, rows] = jnp.dot(
                attended[rows], w_other[:, here], preferred_element_type=F32
            ).astype(BF16)
            part_copy(g, c).start()
        for c in range(COLUMN_CHUNKS):
            here = slice(c * step, (c + 1) * step)
            kept[c, rows] = jnp.dot(attended[rows], w_mine[:, here], preferred_element_type=F32)

    def gather(g, c):
        first, last = bounds[g] * capacity, bounds[g + 1] * capacity
        part_copy(g, c).wait()
        total = kept[c, first:last] + part_got[c, first:last].astype(F32)
        high = total.astype(BF16)
        gained[c, first:last] = high
        gained[c, streams + first : streams + last] = (total - high.astype(F32)).astype(BF16)

    groups = len(bounds) - 1
    for g in range(groups):
        lax.fori_loop(bounds[g], bounds[g + 1], attend, 0)
        if g:
            project(g - 1)
    project(groups - 1)
    residual_copy.wait()
    for g in range(groups - 1):
        for c in range(COLUMN_CHUNKS):
            gather(g, c)
    for c in range(COLUMN_CHUNKS):
        gather(groups - 1, c)
        span = slice(c * step, (c + 1) * step)
        out_ref[:, span] = (
            residual[:, span].astype(F32)
            + jnp.dot(place_back[...], gained[c], preferred_element_type=F32)
        ).astype(BF16)
    for k in range(1, n):
        id_copy(k).wait_send()
        query_copy(k).wait_send()
        back_copy(k).wait_send()
        lse_copy(k).wait_send()


def fused_body(residual, fresh_qkv, active, home_slot, kv_cache, lengths, w_out):
    n = lax.axis_size("dp")
    streams, columns = residual.shape
    width = fresh_qkv.shape[2]
    heads = width // HD
    capacity = streams // n
    quarter = n // 4
    bounds = (0, quarter, 2 * quarter, 3 * quarter, 3 * quarter + quarter // 2, n)
    groups = len(bounds) - 1
    rows = (n, capacity, width)
    lse_rows = (n, 1, heads * capacity)
    step = columns // COLUMN_CHUNKS
    vmem = pl.BlockSpec(memory_space=pltpu.VMEM)
    smem = pl.BlockSpec(memory_space=pltpu.SMEM)
    anywhere = pl.BlockSpec(memory_space=pl.ANY)
    dma = pltpu.SemaphoreType.DMA
    return pl.pallas_call(
        functools.partial(kernel, n, heads, bounds),
        out_shape=pltpu.VMEM((streams, columns), BF16),
        in_specs=[vmem] * 2 + [smem] + [anywhere] * 4,
        out_specs=vmem,
        scratch_shapes=[
            pltpu.VMEM((3, streams, width), BF16),
            pltpu.VMEM(kv_cache.shape, BF16),
            pltpu.VMEM((w_out.shape[0], columns), BF16),
            pltpu.VMEM((w_out.shape[0], columns), BF16),
            pltpu.VMEM(residual.shape, BF16),
            pltpu.VMEM(rows, BF16),
            pltpu.VMEM(rows, BF16),
            pltpu.VMEM((1, streams), jnp.int32),
            pltpu.SMEM((n, 1, streams), jnp.int32),
            pltpu.VMEM(rows, BF16),
            pltpu.VMEM(rows, BF16),
            pltpu.VMEM(lse_rows, F32),
            pltpu.VMEM(lse_rows, F32),
            pltpu.VMEM((streams, LANES), F32),
            pltpu.VMEM((streams, width), BF16),
            pltpu.VMEM((streams, 2 * streams), BF16),
            pltpu.VMEM((streams, width), BF16),
            pltpu.VMEM((COLUMN_CHUNKS, streams, step), BF16),
            pltpu.VMEM((COLUMN_CHUNKS, streams, step), BF16),
            pltpu.VMEM((COLUMN_CHUNKS, streams, step), F32),
            pltpu.VMEM((COLUMN_CHUNKS, 2 * streams, step), BF16),
            dma((3,)),
            dma((KV_PARTS,)),
            dma((2,)),
            dma,
        ]
        + [dma((n,))] * 8
        + [dma((groups, COLUMN_CHUNKS))] * 2,
        compiler_params=pltpu.CompilerParams(
            collective_id=0, has_side_effects=True, vmem_limit_bytes=60 * 1024 * 1024
        ),
    )(
        home_slot.reshape(1, streams),
        active.reshape(1, streams),
        lengths.reshape(1, streams),
        jnp.transpose(fresh_qkv, (1, 0, 2)),
        kv_cache,
        w_out,
        residual,
    )


def body(residual, fresh_qkv, active, home_slot, kv_cache, lengths, w_out):
    n = lax.axis_size("dp")
    streams = home_slot.shape[0]
    heads = fresh_qkv.shape[2] // HD
    fits = (
        lax.axis_size("tensor") == 2
        and n % 8 == 0
        and n & (n - 1) == 0
        and streams == 16 * n
        and streams <= 256
        and heads * 16 == LANES
        and kv_cache.shape[2] == 16
    )
    chosen = fused_body if fits else general_body
    return chosen(residual, fresh_qkv, active, home_slot, kv_cache, lengths, w_out)


def solution(mesh):
    placed = (
        P("dp", "tensor"),
        P("dp", None, "tensor"),
        P("dp"),
        P("dp"),
        P("dp", None, None, "tensor"),
        P("dp"),
        P("tensor", None),
    )
    return jax.shard_map(
        body, mesh=mesh, in_specs=placed, out_specs=P("dp", "tensor"), check_vma=False
    )
```

time: 70.9 us -> 48.3 us (0.68)
  Pallas kernels: 64.9 us -> 47.1 us
  local copies, waits for them, and re-layouts: 5.77 us -> 0.97 us
    pallas_call x1, Pallas kernels: 64.9 us -> 47.1 us  [fused_body(): pl.pallas_call(functools.partial(kernel, n, heads, bounds), out_shape=plt...]
    unnamed x2 -> x1, local copies, waits for them, and re-layouts: 4.01 us -> 0.97 us
    reshape x1 -> x0, local copies, waits for them, and re-layouts: 1.76 us -> none  [fused_body(): fresh_qkv.reshape(streams, 3 * width)]
where the time goes in v1:
time: 48.3 us; the launch traced here: 48.1 us
  Pallas kernels  47.1 us (98%)
  local copies, waits for them, and re-layouts  0.97 us (2%)
    pallas_call x1, Pallas kernels, fused_body(): pl.pallas_call(functools.partial(kernel, n, heads, bounds), out_shape=plt...  47.1 us
    unnamed x1, local copies, waits for them, and re-layouts  0.97 us

profile of v1, /device:TPU:0, one launch (start us, length us, event | category | flops | bytes accessed | tf_op | source)
XLA Modules:
  0.0 48.1 jit_solution(6738541799522845100)
XLA Ops:
  0.0 47.1 %shard_map.73 = bf16[256,2048]{1,0:T(8,128)(2,1)S(1)} custom-call(s32[1,256]{1,0:T(1,128)} %bitcast.5, s32[1,256]{1,0:T(1,128)} %bitcast.6, s32[1,256]{1,0:T(1,128)} %bitcast.7, bf16[3,256,1024]{2,1,0:T(8,128)(2,1)} %bitcast.4, bf16[256,2,16,1024]{3,2,1,0:T(8,128)(2,1)} %kv_hbm.1, bf16[1024,4096]{1,0:T(8,128)(2,1)} %w_hbm.1, bf16[256,2048]{1,0:T(8,128)(2,1)} %residual_hbm.1), custom_call_target="tpu_custom_call" | custom-call | tf_op jit(solution)/shard_map/pallas_call | solution.py:421
  47.2 1.0 %copy.9 = bf16[256,2048]{1,0:T(8,128)(2,1)} copy(bf16[256,2048]{1,0:T(8,128)(2,1)S(1)} %shard_map.73) | data formatting | bytes 2097152

commit v2 on v1

--- a/solution.py
+++ b/solution.py
@@ -108,7 +108,7 @@
 BF16 = jnp.bfloat16
 LANES = 128
 KV_PARTS = 4
-COLUMN_CHUNKS = 4
+COLUMN_CHUNKS = 2
 
 
 def partner_of(me, k, n):
@@ -124,7 +124,7 @@
 
 
 def kernel(
-    n, heads, bounds, home_ref, active_ref, lengths_ref, fresh_hbm, kv_hbm, w_hbm, residual_hbm,
+    n, heads, plan, home_ref, active_ref, lengths_ref, fresh_hbm, kv_hbm, w_hbm, residual_hbm,
     out_ref,
     fresh, kv, w_mine, w_other, residual, send_q, got_q, send_i, ids, send_a, got_a, send_l, got_l,
     own, value_rows, place_back, attended, part_send, part_got, kept, gained,
@@ -170,10 +170,7 @@
         )
         for i, (at, dst) in enumerate(((other, w_other), (side, w_mine)))
     ]
-    for copy in w_copies:
-        copy.start()
     residual_copy = pltpu.make_async_copy(residual_hbm, residual, residual_sem)
-    residual_copy.start()
 
     home = home_ref[...]
     is_active = active_ref[...] > 0
@@ -197,6 +194,9 @@
     )
     send_i[...] = slot_ids[:1].astype(jnp.int32)
     fresh_copies[0].wait()
+    for copy in w_copies:
+        copy.start()
+    residual_copy.start()
     send_q[...] = (
         jnp.dot(placed, fresh[0], preferred_element_type=F32)
         .astype(BF16)
@@ -249,8 +249,6 @@
         own_h = jnp.sum(query * key, axis=1, keepdims=True) * scale
         own_scores = jnp.where(lane == h, own_h, own_scores)
     own[...] = own_scores
-    turned = jnp.transpose(placing).astype(BF16)
-    place_back[...] = jnp.concatenate([turned, turned], axis=1)
     for copy in kv_copies:
         copy.wait()
 
@@ -316,21 +314,19 @@
 
         return carry
 
-    def part_copy(g, c):
-        rows = pl.ds(bounds[g] * capacity, (bounds[g + 1] - bounds[g]) * capacity)
+    def part_copy(first, last, c):
+        rows = pl.ds(first * capacity, (last - first) * capacity)
         return pltpu.make_async_remote_copy(
             src_ref=part_send.at[c, rows],
             dst_ref=part_got.at[c, rows],
-            send_sem=p_send.at[g, c],
-            recv_sem=p_got.at[g, c],
+            send_sem=p_send.at[first, c],
+            recv_sem=p_got.at[first, c],
             device_id=pair,
             device_id_type=MESH,
         )
 
-    def project(g):
-        first, last = bounds[g], bounds[g + 1]
+    def project(first, last):
         rows = slice(first * capacity, last * capacity)
-        count = (last - first) * capacity
         for k in range(first, last):
             if k:
                 back_copy(k).wait_recv()
@@ -338,7 +334,7 @@
             else:
                 back_here.wait()
                 lse_here.wait()
-        arrived = got_a[first:last].reshape(count, width)
+        arrived = got_a[first:last].reshape((last - first) * capacity, width)
         own_rows = own[rows]
         turned = [
             jnp.sum(jnp.where(eye, got_l[k], 0.0), axis=1, keepdims=True)
@@ -357,39 +353,51 @@
                 (from_cache * share) * arrived[:, span].astype(F32)
                 + (from_own * share) * value_rows[rows, span].astype(F32)
             ).astype(BF16)
-        if g == 0:
-            for copy in w_copies:
-                copy.wait()
+        if first == 0:
+            w_copies[0].wait()
         for c in range(COLUMN_CHUNKS):
-            here = slice(c * step, (c + 1) * step)
             part_send[c, rows] = jnp.dot(
-                attended[rows], w_other[:, here], preferred_element_type=F32
+                attended[rows], w_other[:, c * step : (c + 1) * step], preferred_element_type=F32
             ).astype(BF16)
-            part_copy(g, c).start()
+            part_copy(first, last, c).start()
+
+    def keep(first, last):
+        rows = slice(first * capacity, last * capacity)
+        if first == 0:
+            w_copies[1].wait()
         for c in range(COLUMN_CHUNKS):
-            here = slice(c * step, (c + 1) * step)
-            kept[c, rows] = jnp.dot(attended[rows], w_mine[:, here], preferred_element_type=F32)
-
-    def gather(g, c):
-        first, last = bounds[g] * capacity, bounds[g + 1] * capacity
-        part_copy(g, c).wait()
-        total = kept[c, first:last] + part_got[c, first:last].astype(F32)
+            kept[c, rows] = jnp.dot(
+                attended[rows], w_mine[:, c * step : (c + 1) * step], preferred_element_type=F32
+            )
+
+    def gather(first, last, c):
+        rows = slice(first * capacity, last * capacity)
+        for begin, end in sends:
+            if first <= begin < last:
+                part_copy(begin, end, c).wait()
+        total = kept[c, rows] + part_got[c, rows].astype(F32)
         high = total.astype(BF16)
-        gained[c, first:last] = high
-        gained[c, streams + first : streams + last] = (total - high.astype(F32)).astype(BF16)
-
-    groups = len(bounds) - 1
-    for g in range(groups):
-        lax.fori_loop(bounds[g], bounds[g + 1], attend, 0)
-        if g:
-            project(g - 1)
-    project(groups - 1)
+        gained[c, rows] = high
+        gained[c, streams + first * capacity : streams + last * capacity] = (
+            total - high.astype(F32)
+        ).astype(BF16)
+
+    sends = [(first, last) for what, first, last in plan if what == "project"]
+    for what, first, last in plan:
+        if what == "attend":
+            lax.fori_loop(first, last, attend, 0)
+        elif what == "project":
+            project(first, last)
+        else:
+            keep(first, last)
+    turned = jnp.transpose(placing).astype(BF16)
+    place_back[...] = jnp.concatenate([turned, turned], axis=1)
     residual_copy.wait()
-    for g in range(groups - 1):
-        for c in range(COLUMN_CHUNKS):
-            gather(g, c)
+    late = n - n // 4
     for c in range(COLUMN_CHUNKS):
-        gather(groups - 1, c)
+        gather(0, late, c)
+    for c in range(COLUMN_CHUNKS):
+        gather(late, n, c)
         span = slice(c * step, (c + 1) * step)
         out_ref[:, span] = (
             residual[:, span].astype(F32)
@@ -402,15 +410,40 @@
         lse_copy(k).wait_send()
 
 
+def steps_of(n):
+    q = n // 4
+    return (
+        ("attend", 0, 1),
+        ("project", 0, 1),
+        ("attend", 1, q),
+        ("project", 1, 2),
+        ("project", 2, q),
+        ("attend", q, 2 * q),
+        ("keep", 0, q),
+        ("attend", 2 * q, 3 * q),
+        ("project", q, q + 2),
+        ("attend", 3 * q, 3 * q + 1),
+        ("project", q + 2, 2 * q),
+        ("attend", 3 * q + 1, 3 * q + 2),
+        ("project", 2 * q, 2 * q + 2),
+        ("attend", 3 * q + 2, n),
+        ("project", 2 * q + 2, 3 * q),
+        ("keep", q, 2 * q),
+        ("project", 3 * q, 3 * q + 2),
+        ("project", 3 * q + 2, n - 1),
+        ("project", n - 1, n),
+        ("keep", 2 * q, 3 * q),
+        ("keep", 3 * q, n),
+    )
+
+
 def fused_body(residual, fresh_qkv, active, home_slot, kv_cache, lengths, w_out):
     n = lax.axis_size("dp")
     streams, columns = residual.shape
     width = fresh_qkv.shape[2]
     heads = width // HD
     capacity = streams // n
-    quarter = n // 4
-    bounds = (0, quarter, 2 * quarter, 3 * quarter, 3 * quarter + quarter // 2, n)
-    groups = len(bounds) - 1
+    plan = steps_of(n)
     rows = (n, capacity, width)
     lse_rows = (n, 1, heads * capacity)
     step = columns // COLUMN_CHUNKS
@@ -419,7 +452,7 @@
     anywhere = pl.BlockSpec(memory_space=pl.ANY)
     dma = pltpu.SemaphoreType.DMA
     return pl.pallas_call(
-        functools.partial(kernel, n, heads, bounds),
+        functools.partial(kernel, n, heads, plan),
         out_shape=pltpu.VMEM((streams, columns), BF16),
         in_specs=[vmem] * 2 + [smem] + [anywhere] * 4,
         out_specs=vmem,
@@ -451,7 +484,7 @@
             dma,
         ]
         + [dma((n,))] * 8
-        + [dma((groups, COLUMN_CHUNKS))] * 2,
+        + [dma((n, COLUMN_CHUNKS))] * 2,
         compiler_params=pltpu.CompilerParams(
             collective_id=0, has_side_effects=True, vmem_limit_bytes=60 * 1024 * 1024
         ),
@@ -472,7 +505,7 @@
     heads = fresh_qkv.shape[2] // HD
     fits = (
         lax.axis_size("tensor") == 2
-        and n % 8 == 0
+        and n % 16 == 0
         and n & (n - 1) == 0
         and streams == 16 * n
         and streams <= 256

time: 48.3 us -> 47.1 us (0.975)
  Pallas kernels: 47.1 us -> 46 us
    pallas_call x1, Pallas kernels: 47.1 us -> 46 us  [fused_body(): pl.pallas_call(functools.partial(kernel, n, heads, plan), out_shape=pltpu...]
where the time goes in v2:
time: 47.1 us; the launch traced here: 47 us
  Pallas kernels  46 us (98%)
  local copies, waits for them, and re-layouts  0.97 us (2%)
    pallas_call x1, Pallas kernels, fused_body(): pl.pallas_call(functools.partial(kernel, n, heads, plan), out_shape=pltpu...  46 us
    unnamed x1, local copies, waits for them, and re-layouts  0.97 us

profile of v2, /device:TPU:0, one launch (start us, length us, event | category | flops | bytes accessed | tf_op | source)
XLA Modules:
  0.0 47.0 jit_solution(6149858647479367116)
XLA Ops:
  0.0 46.0 %shard_map.73 = bf16[256,2048]{1,0:T(8,128)(2,1)S(1)} custom-call(s32[1,256]{1,0:T(1,128)} %bitcast.5, s32[1,256]{1,0:T(1,128)} %bitcast.6, s32[1,256]{1,0:T(1,128)} %bitcast.7, bf16[3,256,1024]{2,1,0:T(8,128)(2,1)} %bitcast.4, bf16[256,2,16,1024]{3,2,1,0:T(8,128)(2,1)} %kv_hbm.1, bf16[1024,4096]{1,0:T(8,128)(2,1)} %w_hbm.1, bf16[256,2048]{1,0:T(8,128)(2,1)} %residual_hbm.1), custom_call_target="tpu_custom_call" | custom-call | tf_op jit(solution)/shard_map/pallas_call | solution.py:454
  46.0 1.0 %copy.9 = bf16[256,2048]{1,0:T(8,128)(2,1)} copy(bf16[256,2048]{1,0:T(8,128)(2,1)S(1)} %shard_map.73) | data formatting | bytes 2097152

commit v3 on v2

--- a/solution.py
+++ b/solution.py
@@ -428,11 +428,9 @@
         ("project", 2 * q, 2 * q + 2),
         ("attend", 3 * q + 2, n),
         ("project", 2 * q + 2, 3 * q),
-        ("keep", q, 2 * q),
+        ("keep", q, 3 * q),
         ("project", 3 * q, 3 * q + 2),
-        ("project", 3 * q + 2, n - 1),
-        ("project", n - 1, n),
-        ("keep", 2 * q, 3 * q),
+        ("project", 3 * q + 2, n),
         ("keep", 3 * q, n),
     )
 

time: 47.1 us -> 47 us (level)
  no operation moved by 1% of the time
where the time goes in v3:
time: 47 us; the launch traced here: 46.9 us
  Pallas kernels  45.9 us (98%)
  local copies, waits for them, and re-layouts  0.97 us (2%)
    pallas_call x1, Pallas kernels, fused_body(): pl.pallas_call(functools.partial(kernel, n, heads, plan), out_shape=pltpu...  45.9 us
    unnamed x1, local copies, waits for them, and re-layouts  0.97 us

profile of v3, /device:TPU:0, one launch (start us, length us, event | category | flops | bytes accessed | tf_op | source)
XLA Modules:
  0.0 46.9 jit_solution(2868239438675153334)
XLA Ops:
  0.0 45.9 %shard_map.73 = bf16[256,2048]{1,0:T(8,128)(2,1)S(1)} custom-call(s32[1,256]{1,0:T(1,128)} %bitcast.5, s32[1,256]{1,0:T(1,128)} %bitcast.6, s32[1,256]{1,0:T(1,128)} %bitcast.7, bf16[3,256,1024]{2,1,0:T(8,128)(2,1)} %bitcast.4, bf16[256,2,16,1024]{3,2,1,0:T(8,128)(2,1)} %kv_hbm.1, bf16[1024,4096]{1,0:T(8,128)(2,1)} %w_hbm.1, bf16[256,2048]{1,0:T(8,128)(2,1)} %residual_hbm.1), custom_call_target="tpu_custom_call" | custom-call | tf_op jit(solution)/shard_map/pallas_call | solution.py:452
  45.9 1.0 %copy.9 = bf16[256,2048]{1,0:T(8,128)(2,1)} copy(bf16[256,2048]{1,0:T(8,128)(2,1)S(1)} %shard_map.73) | data formatting | bytes 2097152
